TPU v7x, 32 devices: a whole 2x2x4 slice. The times are simulated.
32 devices in a mesh: gx: 8 (over z, y), gy: 4 (over x, core).
Axes of the slice: x: 2, y: 2, z: 4, core: 2. Of those that a mesh axis runs over, the one named last changes fastest.
Arguments:
- probes: bfloat16 [16, 32768], P(None, ('gx', 'gy')), may hold values from -73 to 73, as said below
- previous: bfloat16 [16, 32768], P(None, ('gx', 'gy')), may hold values from -6 to 6
- prev_coupling: float32 [16, 16], replicated, may hold values from -1.5 to 1.5
- leaves: bfloat16 [32, 1024, 1024], P(('gx', 'gy')), may hold values from -1 to 3, as said below
- bases: bfloat16 [5, 64, 32768], P(None, None, ('gx', 'gy')), may hold values from -6 to 6
- leaf_sizes: int32 [32], P(('gx', 'gy')), may hold values from 1 to 1024, 24576 in all
Outputs:
- rayleigh: float32 [16, 16], replicated
- factor: float32 [16, 16], replicated
- next_block: float32 [16, 32768], P(None, ('gx', 'gy'))
Inputs may be any that keep to these rules, and one draw needn't show every extreme that they name: For every probe p and slot s, |probes[p, s]| stays within the range below. Each leaves[i] is symmetric. `leaf_sizes`: the real points of a leaf fill its first slots; the sizes sum to 24576.
All inputs are finite; a program needn't handle non-finite values. No bound on the sum of `leaf_sizes` on one device may be relied on, other than what follows from the above.
Results may differ from a plain program's by a relative error of at most 0.0022.
Values sent between devices are 32-bit elements; how exact they have to be, the bound alone decides.
A program may use at most 64 MiB of HBM per device.

v0:
```python
import math

import jax
import jax.numpy as jnp
from jax import lax
from jax.sharding import PartitionSpec as P


def partner_2(block, axis, stride):
    count = lax.axis_size(axis)
    route = []
    for low in range(count):
        high = low | 1 << stride
        if high != low and high < count:
            route += [(low, high), (high, low)]
    return lax.ppermute(block, axis, route)


def sibling_sums(partials, spread):
    results = []
    for upper_bit in range(spread):
        running = partials[upper_bit]
        for lower_bit in range(upper_bit):
            running = running + partner_2(running, ("gx", "gy"), lower_bit)
        results.append(partner_2(running, ("gx", "gy"), upper_bit))
    return results


def body(probes, previous, prev_coupling, leaves, bases, leaf_sizes):
    highest = lax.Precision.HIGHEST
    probe_count = probes.shape[0]
    leaf_count = leaves.shape[0]
    leaf_rows = leaves.shape[1]
    rows = leaf_count * leaf_rows
    rank = bases.shape[1]
    devices = lax.axis_size(("gx", "gy"))
    spread = devices.bit_length() - 1
    filled = leaf_count * devices * leaf_rows * 3 // 4
    inverse = 1.0 / filled
    valid = (jnp.arange(leaf_rows, dtype=jnp.int32)[None, :] < leaf_sizes[:, None]).reshape(rows)
    block = jnp.where(valid[None, :], probes, jnp.zeros_like(probes))
    older = jnp.where(valid[None, :], previous, jnp.zeros_like(previous))
    shaped = block.reshape(probe_count, leaf_count, leaf_rows)
    image = jnp.einsum("lrc,plc->plr", leaves, shaped, preferred_element_type=jnp.float32).reshape(
        probe_count, rows
    )
    partials = jnp.einsum("pm,krm->kpr", block, bases, preferred_element_type=jnp.float32)
    partners = sibling_sums(partials, spread)
    for bit_number in range(spread):
        width = rows * 2**bit_number
        scaled = (partners[bit_number] * (1.0 / math.sqrt(rank * width))).astype(jnp.bfloat16)
        image = image + jnp.dot(scaled, bases[bit_number], preferred_element_type=jnp.float32)
    image = jnp.where(valid[None, :], image, jnp.zeros_like(image))
    dense = block.astype(jnp.float32)
    older_dense = older.astype(jnp.float32)
    stacked = jnp.concatenate([image, dense, older_dense], 0)
    joint = lax.psum(jnp.dot(stacked, stacked.T, precision=highest) * inverse, ("gx", "gy"))
    rayleigh = joint[probe_count : 2 * probe_count, :probe_count]
    mixing = jnp.concatenate(
        [jnp.eye(probe_count, dtype=jnp.float32), -rayleigh.T, -prev_coupling], 1
    )
    gram = jnp.dot(jnp.dot(mixing, joint, precision=highest), mixing.T, precision=highest)
    residual = (
        image
        - jnp.dot(rayleigh.T, dense, precision=highest)
        - jnp.dot(prev_coupling, older_dense, precision=highest)
    )
    factor = jnp.linalg.cholesky(gram)
    next_block = jax.scipy.linalg.solve_triangular(factor, residual, lower=True)
    return (rayleigh, factor, next_block)


def solution(mesh):
    in_specs = (
        P(None, ("gx", "gy")),
        P(None, ("gx", "gy")),
        P(),
        P(("gx", "gy"), None, None),
        P(None, None, ("gx", "gy")),
        P(("gx", "gy")),
    )
    out_specs = (P(), P(), P(None, ("gx", "gy")))
    return jax.shard_map(body, mesh=mesh, in_specs=in_specs, out_specs=out_specs, check_vma=False)
```

profile of v0, /device:TPU:0, one launch (start us, length us, event | category | flops | bytes accessed | tf_op | source)
XLA Modules:
  0.0 73.7 jit_solution(5655083052039483747)
XLA Ops:
  1.5 1.5 %convolution_bitcast_fusion.1 = f32[5,16,64]{2,1,0:T(8,128)S(1)} fusion(bf16[5,64,1024]{2,1,0:T(8,128)(2,1)} %param.10, bf16[16,1024]{1,0:T(8,128)(2,1)} %param.6, pred[1024]{0:T(1024)(128)(4,1)S(1)} %iota_compare_fusion.2), kind=kOutput, calls=%fused_computation.11 | convolution fusion | flops 10502144 | bytes 709632 | tf_op jit(solution)/shard_map/pm,krm->kpr/dot_general | solution.py:47
  3.0 0.6 collective-permute-start.1
  3.6 0.4 collective-permute-start.3
  4.1 0.4 collective-permute-start
  4.6 1.4 %fusion = f32[16,1024]{1,0:T(8,128)S(1)} fusion(bf16[1,1024,1024]{2,1,0:T(8,128)(2,1)S(1)} %copy-done, bf16[16,1024]{1,0:T(8,128)(2,1)} %param.6, pred[1024]{0:T(1024)(128)(4,1)S(1)} %iota_compare_fusion.2), kind=kOutput, calls=%fused_computation | convolution fusion | flops 33570816 | bytes 2196480 | tf_op jit(solution)/shard_map/lrc,plc->plr/dot_general | solution.py:44
  6.1 2.6 %collective-permute-start.4 = (f32[16,64]{1,0:T(8,128)S(1)}, f32[16,64]{1,0:T(8,128)S(1)}, u32[]{:S(2)}, u32[]{:S(2)}) collective-permute-start(f32[16,64]{1,0:T(8,128)S(1)} %get-tuple-element.11), channel_id=1, source_target_pairs={{0,2},{2,0},{1,3},{3,1},{4,6},{6,4},{5,7},{7,5},{8,10},{10,8},{9,1... | collective-permute-start | bytes 12296 | tf_op jit(solution)/shard_map/ppermute | solution.py:16
  8.8 1.9 %collective-permute-start.11 = (f32[16,64]{1,0:T(8,128)S(1)}, f32[16,64]{1,0:T(8,128)S(1)}, u32[]{:S(2)}, u32[]{:S(2)}) collective-permute-start(f32[16,64]{1,0:T(8,128)S(1)} %get-tuple-element.9), channel_id=1, source_target_pairs={{0,2},{2,0},{1,3},{3,1},{4,6},{6,4},{5,7},{7,5},{8,10},{10,8},{9,1... | collective-permute-start | bytes 12296 | tf_op jit(solution)/shard_map/ppermute | solution.py:16
  10.7 0.1 collective-permute-start.2
  10.9 2.0 %collective-permute-start.5 = (f32[16,64]{1,0:T(8,128)S(1)}, f32[16,64]{1,0:T(8,128)S(1)}, u32[]{:S(2)}, u32[]{:S(2)}) collective-permute-start(f32[16,64]{1,0:T(8,128)S(1)} %add.63), channel_id=1, source_target_pairs={{0,4},{4,0},{1,5},{5,1},{2,6},{6,2},{3,7},{7,3},{8,12},{12,8},{9,1... | collective-permute-start | bytes 12296 | tf_op jit(solution)/shard_map/ppermute | solution.py:16
  12.9 1.0 %collective-permute-start.8 = (f32[16,64]{1,0:T(8,128)S(1)}, f32[16,64]{1,0:T(8,128)S(1)}, u32[]{:S(2)}, u32[]{:S(2)}) collective-permute-start(f32[16,64]{1,0:T(8,128)S(1)} %add.66), channel_id=1, source_target_pairs={{0,4},{4,0},{1,5},{5,1},{2,6},{6,2},{3,7},{7,3},{8,12},{12,8},{9,1... | collective-permute-start | bytes 12296 | tf_op jit(solution)/shard_map/ppermute | solution.py:16
  13.9 1.0 %collective-permute-start.12 = (f32[16,64]{1,0:T(8,128)S(1)}, f32[16,64]{1,0:T(8,128)S(1)}, u32[]{:S(2)}, u32[]{:S(2)}) collective-permute-start(f32[16,64]{1,0:T(8,128)S(1)} %add.70), channel_id=1, source_target_pairs={{0,4},{4,0},{1,5},{5,1},{2,6},{6,2},{3,7},{7,3},{8,12},{12,8},{9,1... | collective-permute-start | bytes 12296 | tf_op jit(solution)/shard_map/ppermute | solution.py:16
  14.9 0.1 convolution_add_fusion.1
  15.1 1.5 %collective-permute-done.8 = f32[16,64]{1,0:T(8,128)S(1)} collective-permute-done((f32[16,64]{1,0:T(8,128)S(1)}, f32[16,64]{1,0:T(8,128)S(1)}, u32[]{:S(2)}, u32[]{:S(2)}) %collective-permute-start.8) | collective-permute-done | bytes 4128 | tf_op jit(solution)/shard_map/ppermute | solution.py:16
  16.5 1.6 %collective-permute-start.9 = (f32[16,64]{1,0:T(8,128)S(1)}, f32[16,64]{1,0:T(8,128)S(1)}, u32[]{:S(2)}, u32[]{:S(2)}) collective-permute-start(f32[16,64]{1,0:T(8,128)S(1)} %add.67), channel_id=1, source_target_pairs={{0,8},{8,0},{1,9},{9,1},{2,10},{10,2},{3,11},{11,3},{4,12},{12,4},... | collective-permute-start | bytes 12296 | tf_op jit(solution)/shard_map/ppermute | solution.py:16
  18.1 1.0 %collective-permute-start.13 = (f32[16,64]{1,0:T(8,128)S(1)}, f32[16,64]{1,0:T(8,128)S(1)}, u32[]{:S(2)}, u32[]{:S(2)}) collective-permute-start(f32[16,64]{1,0:T(8,128)S(1)} %add.71), channel_id=1, source_target_pairs={{0,8},{8,0},{1,9},{9,1},{2,10},{10,2},{3,11},{11,3},{4,12},{12,4},... | collective-permute-start | bytes 12296 | tf_op jit(solution)/shard_map/ppermute | solution.py:16
  19.1 0.1 fusion.16
  19.3 2.5 %collective-permute-done.13 = f32[16,64]{1,0:T(8,128)S(1)} collective-permute-done((f32[16,64]{1,0:T(8,128)S(1)}, f32[16,64]{1,0:T(8,128)S(1)}, u32[]{:S(2)}, u32[]{:S(2)}) %collective-permute-start.13) | collective-permute-done | bytes 4128 | tf_op jit(solution)/shard_map/ppermute | solution.py:16
  21.8 2.6 %collective-permute-start.14 = (f32[16,64]{1,0:T(8,128)S(1)}, f32[16,64]{1,0:T(8,128)S(1)}, u32[]{:S(2)}, u32[]{:S(2)}) collective-permute-start(f32[16,64]{1,0:T(8,128)S(1)} %add.72), channel_id=1, source_target_pairs={{0,16},{16,0},{1,17},{17,1},{2,18},{18,2},{3,19},{19,3},{4,20},{20... | collective-permute-start | bytes 12296 | tf_op jit(solution)/shard_map/ppermute | solution.py:16
  24.5 1.8 %collective-permute-done.14 = f32[16,64]{1,0:T(8,128)S(1)} collective-permute-done((f32[16,64]{1,0:T(8,128)S(1)}, f32[16,64]{1,0:T(8,128)S(1)}, u32[]{:S(2)}, u32[]{:S(2)}) %collective-permute-start.14) | collective-permute-done | bytes 4128 | tf_op jit(solution)/shard_map/ppermute | solution.py:16
  26.5 0.1 fusion.6
  26.6 0.3 convolution_multiply_fusion
  26.9 39.6 %psum.7 = f32[48,48]{0,1:T(8,128)S(1)} all-reduce(f32[48,48]{0,1:T(8,128)S(1)} %convolution_multiply_fusion), channel_id=1, replica_groups=mesh['gx'=8,'gy'=4] {'gx','gy'}, use_global_device_ids=true, to_apply=%region_0.1 | all-reduce | flops 2304 | bytes 18432 | tf_op jit(solution)/shard_map/psum | solution.py:57
  66.6 0.2 convolution_subtract_fusion
  66.9 0.2 fusion.2
  67.0 0.2 fusion.57
  67.2 0.2 fusion.56
  67.5 1.5 %cholesky.20 = f32[16,16]{1,0:T(8,128)S(1)} custom-call(f32[16,16]{1,0:T(8,128)S(1)} %fusion.34), custom_call_target="Cholesky" | custom-call | tf_op jit(solution)/shard_map/jit(cholesky)/cholesky | solution.py:68
  69.0 0.6 compare_reduce_fusion
  69.7 1.2 %select_bitcast_fusion = (f32[1,16,16]{2,1,0:T(8,128)S(1)}, f32[16,16]{1,0:T(8,128)}) fusion(f32[16,16]{1,0:T(8,128)S(1)} %cholesky.20, pred[]{:T(512)} %compare_reduce_fusion), kind=kLoop, calls=%fused_computation.50 | loop fusion | flops 1024 | bytes 3073 | tf_op jit(solution)/shard_map/jit(_solve_triangular)/triangular_solve | solution.py:69
  70.9 1.2 %custom-call.7 = f32[1,16,16]{1,2,0:T(8,128)S(1)} custom-call(f32[1,16,16]{2,1,0:T(8,128)S(1)} %get-tuple-element.6), custom_call_target="InvertDiagBlocksLowerTriangular" | custom-call | tf_op jit(solution)/shard_map/jit(_solve_triangular)/triangular_solve | solution.py:69
  72.2 0.7 copy.11
  72.8 0.9 %fusion.32 = f32[16,1024]{1,0:T(8,128)} fusion(f32[16,1024]{1,0:T(8,128)S(1)} %fusion.2, f32[1,16,16]{1,2,0:T(8,128)S(1)} %custom-call.7), kind=kOutput, calls=%fused_computation.46 | convolution fusion | flops 3145728 | bytes 132096 | tf_op jit(solution)/shard_map/jit(_solve_triangular)/triangular_solve | solution.py:69
  (43 shorter events, 0.8 us)
Async XLA Ops:
  0.6 3.9 %copy-start = (bf16[1,1024,1024]{2,1,0:T(8,128)(2,1)S(1)}, bf16[1,1024,1024]{2,1,0:T(8,128)(2,1)}, u32[]{:S(2)}) copy-start(bf16[1,1024,1024]{2,1,0:T(8,128)(2,1)} %param.9) | copy-start | bytes 6291460
  0.6 14.3 %copy-start.1 = (bf16[5,64,1024]{2,1,0:T(8,128)(2,1)S(1)}, bf16[5,64,1024]{2,1,0:T(8,128)(2,1)}, u32[]{:S(2)}) copy-start(bf16[5,64,1024]{2,1,0:T(8,128)(2,1)} %param.10) | copy-start | bytes 1966084
  0.7 5.3 %copy-start.2 = (bf16[16,1024]{1,0:T(8,128)(2,1)S(1)}, bf16[16,1024]{1,0:T(8,128)(2,1)}, u32[]{:S(2)}) copy-start(bf16[16,1024]{1,0:T(8,128)(2,1)} %param.6) | copy-start | bytes 98308
  0.7 5.3 %copy-start.3 = (bf16[16,1024]{1,0:T(8,128)(2,1)S(1)}, bf16[16,1024]{1,0:T(8,128)(2,1)}, u32[]{:S(2)}) copy-start(bf16[16,1024]{1,0:T(8,128)(2,1)} %param.7) | copy-start | bytes 98308
  0.7 10.1 %copy-start.4 = (f32[16,16]{1,0:T(8,128)S(1)}, f32[16,16]{1,0:T(8,128)}, u32[]{:S(2)}) copy-start(f32[16,16]{1,0:T(8,128)} %param.8) | copy-start | bytes 3076
  3.0 3.0 %collective-permute-start.1 = (f32[16,64]{1,0:T(8,128)S(1)}, f32[16,64]{1,0:T(8,128)S(1)}, u32[]{:S(2)}, u32[]{:S(2)}) collective-permute-start(f32[16,64]{1,0:T(8,128)S(1)} %get-tuple-element.12), channel_id=1, source_target_pairs={{0,1},{1,0},{2,3},{3,2},{4,5},{5,4},{6,7},{7,6},{8,9},{9,8},{10,11... | collective-permute-start | bytes 12296 | tf_op jit(solution)/shard_map/ppermute | solution.py:16
  3.6 2.5 %collective-permute-start.10 = (f32[16,64]{1,0:T(8,128)S(1)}, f32[16,64]{1,0:T(8,128)S(1)}, u32[]{:S(2)}, u32[]{:S(2)}) collective-permute-start(f32[16,64]{1,0:T(8,128)S(1)} %get-tuple-element.13), channel_id=1, source_target_pairs={{0,1},{1,0},{2,3},{3,2},{4,5},{5,4},{6,7},{7,6},{8,9},{9,8},{10,11... | collective-permute-start | bytes 12296 | tf_op jit(solution)/shard_map/ppermute | solution.py:16
  3.6 2.4 %collective-permute-start.3 = (f32[16,64]{1,0:T(8,128)S(1)}, f32[16,64]{1,0:T(8,128)S(1)}, u32[]{:S(2)}, u32[]{:S(2)}) collective-permute-start(f32[16,64]{1,0:T(8,128)S(1)} %get-tuple-element.15), channel_id=1, source_target_pairs={{0,1},{1,0},{2,3},{3,2},{4,5},{5,4},{6,7},{7,6},{8,9},{9,8},{10,11... | collective-permute-start | bytes 12296 | tf_op jit(solution)/shard_map/ppermute | solution.py:16
  4.1 2.0 %collective-permute-start.6 = (f32[16,64]{1,0:T(8,128)S(1)}, f32[16,64]{1,0:T(8,128)S(1)}, u32[]{:S(2)}, u32[]{:S(2)}) collective-permute-start(f32[16,64]{1,0:T(8,128)S(1)} %get-tuple-element.14), channel_id=1, source_target_pairs={{0,1},{1,0},{2,3},{3,2},{4,5},{5,4},{6,7},{7,6},{8,9},{9,8},{10,11... | collective-permute-start | bytes 12296 | tf_op jit(solution)/shard_map/ppermute | solution.py:16
  4.1 10.8 %collective-permute-start = (f32[16,64]{1,0:T(8,128)S(1)}, f32[16,64]{1,0:T(8,128)S(1)}, u32[]{:S(2)}, u32[]{:S(2)}) collective-permute-start(f32[16,64]{1,0:T(8,128)S(1)} %get-tuple-element.16), channel_id=1, source_target_pairs={{0,1},{1,0},{2,3},{3,2},{4,5},{5,4},{6,7},{7,6},{8,9},{9,8},{10,11... | collective-permute-start | bytes 12296 | tf_op jit(solution)/shard_map/ppermute | solution.py:16
  6.1 4.8 %collective-permute-start.4 = (f32[16,64]{1,0:T(8,128)S(1)}, f32[16,64]{1,0:T(8,128)S(1)}, u32[]{:S(2)}, u32[]{:S(2)}) collective-permute-start(f32[16,64]{1,0:T(8,128)S(1)} %get-tuple-element.11), channel_id=1, source_target_pairs={{0,2},{2,0},{1,3},{3,1},{4,6},{6,4},{5,7},{7,5},{8,10},{10,8},{9,1... | collective-permute-start | bytes 12296 | tf_op jit(solution)/shard_map/ppermute | solution.py:16
  8.7 4.2 %collective-permute-start.7 = (f32[16,64]{1,0:T(8,128)S(1)}, f32[16,64]{1,0:T(8,128)S(1)}, u32[]{:S(2)}, u32[]{:S(2)}) collective-permute-start(f32[16,64]{1,0:T(8,128)S(1)} %get-tuple-element.10), channel_id=1, source_target_pairs={{0,2},{2,0},{1,3},{3,1},{4,6},{6,4},{5,7},{7,5},{8,10},{10,8},{9,1... | collective-permute-start | bytes 12296 | tf_op jit(solution)/shard_map/ppermute | solution.py:16
  8.8 5.1 %collective-permute-start.11 = (f32[16,64]{1,0:T(8,128)S(1)}, f32[16,64]{1,0:T(8,128)S(1)}, u32[]{:S(2)}, u32[]{:S(2)}) collective-permute-start(f32[16,64]{1,0:T(8,128)S(1)} %get-tuple-element.9), channel_id=1, source_target_pairs={{0,2},{2,0},{1,3},{3,1},{4,6},{6,4},{5,7},{7,5},{8,10},{10,8},{9,1... | collective-permute-start | bytes 12296 | tf_op jit(solution)/shard_map/ppermute | solution.py:16
  10.7 15.7 %collective-permute-start.2 = (f32[16,64]{1,0:T(8,128)S(1)}, f32[16,64]{1,0:T(8,128)S(1)}, u32[]{:S(2)}, u32[]{:S(2)}) collective-permute-start(f32[16,64]{1,0:T(8,128)S(1)} %get-tuple-element.8), channel_id=1, source_target_pairs={{0,2},{2,0},{1,3},{3,1},{4,6},{6,4},{5,7},{7,5},{8,10},{10,8},{9,1... | collective-permute-start | bytes 12296 | tf_op jit(solution)/shard_map/ppermute | solution.py:16
  10.9 8.2 %collective-permute-start.5 = (f32[16,64]{1,0:T(8,128)S(1)}, f32[16,64]{1,0:T(8,128)S(1)}, u32[]{:S(2)}, u32[]{:S(2)}) collective-permute-start(f32[16,64]{1,0:T(8,128)S(1)} %add.63), channel_id=1, source_target_pairs={{0,4},{4,0},{1,5},{5,1},{2,6},{6,2},{3,7},{7,3},{8,12},{12,8},{9,1... | collective-permute-start | bytes 12296 | tf_op jit(solution)/shard_map/ppermute | solution.py:16
  12.9 3.7 %collective-permute-start.8 = (f32[16,64]{1,0:T(8,128)S(1)}, f32[16,64]{1,0:T(8,128)S(1)}, u32[]{:S(2)}, u32[]{:S(2)}) collective-permute-start(f32[16,64]{1,0:T(8,128)S(1)} %add.66), channel_id=1, source_target_pairs={{0,4},{4,0},{1,5},{5,1},{2,6},{6,2},{3,7},{7,3},{8,12},{12,8},{9,1... | collective-permute-start | bytes 12296 | tf_op jit(solution)/shard_map/ppermute | solution.py:16
  13.9 4.2 %collective-permute-start.12 = (f32[16,64]{1,0:T(8,128)S(1)}, f32[16,64]{1,0:T(8,128)S(1)}, u32[]{:S(2)}, u32[]{:S(2)}) collective-permute-start(f32[16,64]{1,0:T(8,128)S(1)} %add.70), channel_id=1, source_target_pairs={{0,4},{4,0},{1,5},{5,1},{2,6},{6,2},{3,7},{7,3},{8,12},{12,8},{9,1... | collective-permute-start | bytes 12296 | tf_op jit(solution)/shard_map/ppermute | solution.py:16
  16.5 7.8 %collective-permute-start.9 = (f32[16,64]{1,0:T(8,128)S(1)}, f32[16,64]{1,0:T(8,128)S(1)}, u32[]{:S(2)}, u32[]{:S(2)}) collective-permute-start(f32[16,64]{1,0:T(8,128)S(1)} %add.67), channel_id=1, source_target_pairs={{0,8},{8,0},{1,9},{9,1},{2,10},{10,2},{3,11},{11,3},{4,12},{12,4},... | collective-permute-start | bytes 12296 | tf_op jit(solution)/shard_map/ppermute | solution.py:16
  18.1 3.7 %collective-permute-start.13 = (f32[16,64]{1,0:T(8,128)S(1)}, f32[16,64]{1,0:T(8,128)S(1)}, u32[]{:S(2)}, u32[]{:S(2)}) collective-permute-start(f32[16,64]{1,0:T(8,128)S(1)} %add.71), channel_id=1, source_target_pairs={{0,8},{8,0},{1,9},{9,1},{2,10},{10,2},{3,11},{11,3},{4,12},{12,4},... | collective-permute-start | bytes 12296 | tf_op jit(solution)/shard_map/ppermute | solution.py:16
  21.8 4.5 %collective-permute-start.14 = (f32[16,64]{1,0:T(8,128)S(1)}, f32[16,64]{1,0:T(8,128)S(1)}, u32[]{:S(2)}, u32[]{:S(2)}) collective-permute-start(f32[16,64]{1,0:T(8,128)S(1)} %add.72), channel_id=1, source_target_pairs={{0,16},{16,0},{1,17},{17,1},{2,18},{18,2},{3,19},{19,3},{4,20},{20... | collective-permute-start | bytes 12296 | tf_op jit(solution)/shard_map/ppermute | solution.py:16
where the time goes:
time: 74.1 us; the launch traced here: 73.7 us
  blocking collectives  39.6 us (53%)
  starting transfers between devices  15.5 us (21%)
  waiting for transfers between devices  5.84 us (8%)
  matrix products  5.56 us (8%)
  other arithmetic  4.77 us (6%)
  between operations  1.59 us (2%)
  local copies, waits for them, and re-layouts  0.79 us (1%)
    psum x1, blocking collectives, body(): lax.psum(jnp.dot(stacked, stacked.T, precision=highest) * inverse, ('gx',...  39.6 us
    ppermute x15, starting transfers between devices, partner_2(): return lax.ppermute(block, axis, route)  15.5 us
    ppermute x15, waiting for transfers between devices, partner_2(): return lax.ppermute(block, axis, route)  5.84 us
    another operation x2, other arithmetic, body(): next_block = jax.scipy.linalg.solve_triangular(factor, residual, lower=True)  2.47 us
    another operation x3, other arithmetic, body(): factor = jnp.linalg.cholesky(gram)  2.15 us
  transfers between devices with their start and end apart: 15, of which 3 were waited for; matrix products, arithmetic and copies ran while one was open for 3% of the time, Pallas kernels for 0%

commit v1 on v0

v1 whole, which is shorter than its diff:
```python
import functools
import math

import jax
import jax.numpy as jnp
from jax import lax
from jax.experimental import pallas as pl
from jax.experimental.pallas import tpu as pltpu
from jax.sharding import PartitionSpec as P

MESH = pl.DeviceIdType.MESH
F32 = jnp.float32
BF16 = jnp.bfloat16
NT = (((1,), (1,)), ((), ()))


def stages_of(spread):
    cuts = [0, min(3, spread)]
    while cuts[-1] < spread:
        cuts.append(min(cuts[-1] + 2, spread))
    return list(zip(cuts[:-1], cuts[1:]))


def tree(values):
    while len(values) > 1:
        values = [a + b for a, b in zip(values[::2], values[1::2])]
    return values[0]


def split3(value):
    high = value.astype(BF16)
    rest = value - high.astype(F32)
    middle = rest.astype(BF16)
    low = (rest - middle.astype(F32)).astype(BF16)
    return high, middle, low


def small_dot(a, b, transposed=False):
    dims = NT if transposed else (((1,), (0,)), ((), ()))
    return lax.dot_general(
        a, b, dims, precision=lax.Precision.HIGHEST, preferred_element_type=F32
    )


def kernel(
    spread, width, inverse,
    probes_hbm, previous_hbm, coupling_hbm, leaves_hbm, bases_hbm, sizes_hbm,
    rayleigh_ref, factor_ref, next_ref,
    probes, previous, coupling, leaves, bases, sizes, wide, local_sems, *rest,
):
    stages = stages_of(spread)
    count = len(stages)
    levels = spread
    runs, lands = rest[:count], rest[count : 2 * count]
    own2, land2 = rest[2 * count : 3 * count], rest[3 * count : 4 * count]
    sems = rest[4 * count :]
    send1, recv1, send2, recv2 = (sems[i * count : (i + 1) * count] for i in range(4))
    p_count, rows = probes.shape
    rank = bases.shape[1]
    half = p_count // 2

    me = lax.axis_index("gx") * width + lax.axis_index("gy")

    def device(mask):
        target = me
        for bit in range(spread):
            if mask >> bit & 1:
                target = target + (1 - 2 * (me // 2**bit % 2)) * 2**bit
        return (target // width, target % width)

    loads = []
    for i, (src, dst) in enumerate(
        [(sizes_hbm, sizes), (probes_hbm, probes), (bases_hbm, bases),
         (leaves_hbm, leaves), (previous_hbm, previous), (coupling_hbm, coupling)]
    ):
        load = pltpu.make_async_copy(src, dst, local_sems.at[i])
        load.start()
        loads.append(load)

    barrier = pltpu.get_barrier_semaphore()
    greeted = 0
    for low, high in stages:
        for m in range(1, 2 ** (high - low)):
            pl.semaphore_signal(barrier, inc=1, device_id=device(m << low), device_id_type=MESH)
            greeted += 1

    loads[0].wait()
    loads[1].wait()
    valid = lax.broadcasted_iota(jnp.int32, (p_count, rows), 1) < sizes[0]
    block = jnp.where(valid, probes[...].astype(F32), 0.0).astype(BF16)
    loads[2].wait()
    for level in range(levels):
        part = lax.dot_general(block, bases[level], NT, preferred_element_type=F32)
        runs[0][level] = jnp.concatenate([part[:half], part[half:]], axis=1)
    pl.semaphore_wait(barrier, greeted)

    def send_stage1(s):
        low, high = stages[s]
        copies = []
        for m in reversed(range(1, 2 ** (high - low))):
            top = low + m.bit_length() - 1
            pieces = [(top, 1, 0)]
            if high < levels:
                pieces.append((high, levels - high, 1))
            for src, size, dst in pieces:
                copy = pltpu.make_async_remote_copy(
                    src_ref=runs[s].at[pl.ds(src, size)],
                    dst_ref=lands[s].at[m - 1, pl.ds(dst, size)],
                    send_sem=send1[s].at[m - 1, min(dst, 1)],
                    recv_sem=recv1[s].at[m - 1, min(dst, 1)],
                    device_id=device(m << low),
                    device_id_type=MESH,
                )
                copy.start()
                copies.append(copy)
        return copies

    def scaled_partners(s):
        low, high = stages[s]
        found = []
        for t in range(low, high):
            b = t - low
            total = tree([lands[s][m - 1, 0] for m in range(2**b, 2 ** (b + 1))])
            total = total * (1.0 / math.sqrt(rank * rows * 2**t))
            found.append(jnp.concatenate([total[:, :rank], total[:, rank:]], axis=0).astype(BF16))
        return found

    copies = send_stage1(0)
    loads[4].wait()
    older = jnp.where(valid, previous[...].astype(F32), 0.0).astype(BF16)
    wide[3 * p_count : 4 * p_count, :] = block
    wide[4 * p_count : 5 * p_count, :] = older
    pair = wide[3 * p_count : 5 * p_count, :]
    early_b = lax.dot_general(block, pair, NT, preferred_element_type=F32)
    early_o = lax.dot_general(older, older, NT, preferred_element_type=F32)
    loads[3].wait()
    image = jnp.dot(block, leaves[0], preferred_element_type=F32)
    for s in range(count):
        low, high = stages[s]
        for copy in copies:
            copy.wait()
        if s + 1 < count:
            for t in range(high, levels):
                runs[s + 1][t] = tree(
                    [runs[s][t]]
                    + [lands[s][m - 1, 1 + t - high] for m in range(1, 2 ** (high - low))]
                )
            copies = send_stage1(s + 1)
        for t, scaled in zip(range(low, high), scaled_partners(s)):
            image = image + jnp.dot(scaled, bases[t], preferred_element_type=F32)
    image = jnp.where(valid, image, 0.0)
    high, middle, lowest = split3(image)
    wide[0:p_count, :] = high
    wide[p_count : 2 * p_count, :] = middle
    wide[2 * p_count : 3 * p_count, :] = lowest
    products = lax.dot_general(
        wide[0 : 3 * p_count, :], wide[...], NT, preferred_element_type=F32
    )
    products = (
        products[:p_count] + products[p_count : 2 * p_count] + products[2 * p_count :]
    )
    own2[0][...] = jnp.concatenate([products, early_b, early_o], axis=1)
    for s in range(count):
        low, top = stages[s]
        copies = []
        for m in reversed(range(1, 2 ** (top - low))):
            copy = pltpu.make_async_remote_copy(
                src_ref=own2[s],
                dst_ref=land2[s].at[m - 1],
                send_sem=send2[s].at[m - 1],
                recv_sem=recv2[s].at[m - 1],
                device_id=device(m << low),
                device_id_type=MESH,
            )
            copy.start()
            copies.append(copy)
        for copy in copies:
            copy.wait()
        total = tree([own2[s][...]] + [land2[s][m - 1] for m in range(1, 2 ** (top - low))])
        if s + 1 < count:
            own2[s + 1][...] = total
    total = total * inverse
    q = p_count
    square = total[:, :q] + total[:, q : 2 * q] + total[:, 2 * q : 3 * q]
    crossed = total[:, 3 * q : 5 * q]
    turned = total[:, 3 * q : 4 * q]
    loads[5].wait()
    mix = coupling[...]
    bb_bo = total[:, 5 * q : 7 * q]
    bo = total[:, 6 * q : 7 * q]
    oo = total[:, 7 * q : 8 * q]
    both = jnp.concatenate([turned, mix], axis=1)
    lower_part = jnp.concatenate([small_dot(mix, bo, True), small_dot(mix, oo)], axis=1)
    u = small_dot(turned, bb_bo) + lower_part
    gram = square - small_dot(both, crossed, True) + small_dot(u - crossed, both, True)
    row_ids = lax.broadcasted_iota(jnp.int32, (q, q), 0)
    lane_ids = lax.broadcasted_iota(jnp.int32, (q, q), 1)
    eye = jnp.where(row_ids == lane_ids, 1.0, 0.0).astype(F32)
    rayleigh_ref[...] = small_dot(eye, turned, True)
    work = jnp.concatenate([gram, eye, eye, eye, -turned, -mix], axis=1)
    factor = jnp.zeros((q, q), F32)
    wide_rows = lax.broadcasted_iota(jnp.int32, work.shape, 0)
    done = jnp.zeros_like(work)
    for k in range(q):
        scale = lax.rsqrt(work[k : k + 1, k : k + 1])
        row = work[k : k + 1, :] * scale
        column = work[:, k : k + 1] * scale
        factor = jnp.where((lane_ids == k) & (row_ids >= k), column, factor)
        done = jnp.where(wide_rows == k, row, done)
        work = work - column * row
    factor_ref[...] = factor
    mixing = done[:, q:]
    pieces = jnp.concatenate(list(split3(mixing)), axis=0)
    result = jnp.dot(pieces, wide[...], preferred_element_type=F32)
    next_ref[...] = result[:q] + result[q : 2 * q] + result[2 * q :]


def body(probes, previous, prev_coupling, leaves, bases, leaf_sizes):
    p_count, rows = probes.shape
    devices = lax.axis_size(("gx", "gy"))
    spread = devices.bit_length() - 1
    filled = devices * rows * 3 // 4
    stages = stages_of(spread)
    rank = bases.shape[1]
    tile = (p_count // 2, 2 * rank)
    lanes = 8 * p_count
    peers = [2 ** (high - low) - 1 for low, high in stages]
    dma = pltpu.SemaphoreType.DMA
    scratch = [
        pltpu.VMEM(probes.shape, BF16),
        pltpu.VMEM(previous.shape, BF16),
        pltpu.VMEM(prev_coupling.shape, F32),
        pltpu.VMEM(leaves.shape, BF16),
        pltpu.VMEM(bases.shape, BF16),
        pltpu.SMEM(leaf_sizes.shape, jnp.int32),
        pltpu.VMEM((5 * p_count, rows), BF16),
        dma((6,)),
    ]
    scratch += [pltpu.VMEM((spread,) + tile, F32) for _ in stages]
    scratch += [
        pltpu.VMEM((n, 1 + spread - high) + tile, F32) for n, (_, high) in zip(peers, stages)
    ]
    scratch += [pltpu.VMEM((p_count, lanes), F32) for _ in stages]
    scratch += [pltpu.VMEM((n, p_count, lanes), F32) for n in peers]
    scratch += [dma((n, 2)) for n in peers] * 2 + [dma((n,)) for n in peers] * 2
    return pl.pallas_call(
        functools.partial(kernel, spread, lax.axis_size("gy"), 1.0 / filled),
        out_shape=[
            jax.ShapeDtypeStruct((p_count, p_count), F32),
            jax.ShapeDtypeStruct((p_count, p_count), F32),
            jax.ShapeDtypeStruct((p_count, rows), F32),
        ],
        in_specs=[pl.BlockSpec(memory_space=pl.ANY)] * 6,
        out_specs=[pl.BlockSpec(memory_space=pltpu.VMEM)] * 3,
        scratch_shapes=scratch,
        compiler_params=pltpu.CompilerParams(collective_id=0, has_side_effects=True),
    )(probes, previous, prev_coupling, leaves, bases, leaf_sizes)


def solution(mesh):
    in_specs = (
        P(None, ("gx", "gy")),
        P(None, ("gx", "gy")),
        P(),
        P(("gx", "gy"), None, None),
        P(None, None, ("gx", "gy")),
        P(("gx", "gy")),
    )
    out_specs = (P(), P(), P(None, ("gx", "gy")))
    return jax.shard_map(body, mesh=mesh, in_specs=in_specs, out_specs=out_specs, check_vma=False)
```

time: 74.1 us -> 28.6 us (0.39)
  blocking collectives: 39.6 us -> 0 us
  Pallas kernels: 0 us -> 22.9 us
  starting transfers between devices: 15.5 us -> 0 us
  waiting for transfers between devices: 5.84 us -> 0 us
  matrix products: 5.56 us -> 0 us
  other arithmetic: 4.77 us -> 0 us
  local copies, waits for them, and re-layouts: 0.79 us -> 4.06 us
    psum x1 -> x0, blocking collectives: 39.6 us -> none  [body(): lax.psum(jnp.dot(stacked, stacked.T, precision=highest) * inverse, ('gx',...]
    pallas_call x0 -> x1, Pallas kernels: none -> 22.9 us  [body(): pl.pallas_call(functools.partial(kernel, spread, lax.axis_size('gy'), 1.0...]
    ppermute x15 -> x0, starting transfers between devices: 15.5 us -> none  [partner_2(): return lax.ppermute(block, axis, route)]
    ppermute x15 -> x0, waiting for transfers between devices: 5.84 us -> none  [partner_2(): return lax.ppermute(block, axis, route)]
    dot_general x12 -> x0, matrix products: 4.67 us -> none  [the longest x1 1.48 us: body(): jnp.einsum('pm,krm->kpr', block, bases, preferred_element_type=jnp.float32)]
    another operation x5 -> x0, other arithmetic: 4.62 us -> none  [the longest x2 2.47 us: body(): next_block = jax.scipy.linalg.solve_triangular(factor, residual, lower=True)]
    unnamed x11 -> x3, local copies, waits for them, and re-layouts: 0.71 us -> 4.06 us
    another operation x1 -> x0, matrix products: 0.88 us -> none  [body(): next_block = jax.scipy.linalg.solve_triangular(factor, residual, lower=True)]
  transfers between devices with their start and end apart: 15 -> 0, of which waited for: 3 -> 0; matrix products, arithmetic and copies ran while one was open for 3% -> 0% of each run, Pallas kernels for 0% -> 0%
where the time goes in v1:
time: 28.6 us; the launch traced here: 28.3 us
  Pallas kernels  22.9 us (80%)
  local copies, waits for them, and re-layouts  4.06 us (14%)
  between operations  1.29 us (5%)
    pallas_call x1, Pallas kernels, body(): pl.pallas_call(functools.partial(kernel, spread, lax.axis_size('gy'), 1.0...  22.9 us
    unnamed x3, local copies, waits for them, and re-layouts  4.06 us

profile of v1, /device:TPU:0, one launch (start us, length us, event | category | flops | bytes accessed | tf_op | source)
XLA Modules:
  0.0 28.3 jit_solution(3555163169208523754)
XLA Ops:
  1.3 22.9 %shard_map.85 = (f32[16,16]{1,0:T(8,128)}, f32[16,16]{1,0:T(8,128)}, f32[16,1024]{1,0:T(8,128)}) custom-call(bf16[16,1024]{1,0:T(8,128)(2,1)} %probes_hbm.1, bf16[16,1024]{1,0:T(8,128)(2,1)} %previous_hbm.1, f32[16,16]{1,0:T(8,128)} %coupling_hbm.1, bf16[1,1024,1024]{2,1,0:T(8,128)(2,1)} %leaves_hbm.1, bf16[5,64,1024]{2,1,0:T(8,128)(2,1)} %bases_hbm.1, ...), custom_call_target="tpu_custom_call" | custom-call | tf_op jit(solution)/shard_map/pallas_call | solution.py:246
  24.2 1.3 %copy.13 = f32[16,16]{1,0:T(8,128)} copy(f32[16,16]{1,0:T(8,128)} %get-tuple-element.6) | data formatting | bytes 2048
  25.5 1.3 %copy.14 = f32[16,16]{1,0:T(8,128)} copy(f32[16,16]{1,0:T(8,128)} %get-tuple-element.7) | data formatting | bytes 2048
  26.8 1.5 %copy.15 = f32[16,1024]{1,0:T(8,128)} copy(f32[16,1024]{1,0:T(8,128)} %get-tuple-element.8) | data formatting | bytes 131072
